TPU v7x, 32 devices: a whole 2x2x4 slice. The times are simulated.
32 devices in a mesh: grp: 4 (over y, core), rep: 8 (over z, x).
Axes of the slice: x: 2, y: 2, z: 4, core: 2. Of those that a mesh axis runs over, the one named last changes fastest.
Arguments:
- embeddings: bfloat16 [16384, 768], P(('grp', 'rep')), may hold values from -6 to 6
- cluster_ids: int32 [16384], P(('grp', 'rep')), may hold values from 0 to 12287, as said below
- owner_bounds: int32 [32], replicated, may hold values from 0 to 12287, as said below
Outputs:
- distance: float32 [16384], P(('grp', 'rep'))
- slot_index: int32 [16384], P(('grp', 'rep'))
- centroids: bfloat16 [32, 576, 768], P(('grp', 'rep'))
Inputs may be any that keep to these rules, and one draw needn't show every extreme that they name: `cluster_ids`: in the rows of one device at most 48 rows belong to the clusters of one owner (owner o holds clusters owner_bounds[o] up to the next bound); in every draw some owner gets exactly 48 rows from every device. `owner_bounds`: owners are ordered grp first, then rep. The bounds rise from 0; each owner holds from 192 to 576 clusters, the last owner ending at 12288; some owner holds exactly 576.
All inputs are finite; a program needn't handle non-finite values.
Results may differ from a plain program's by a relative error of at most 0.004.
Values may be sent and summed in bfloat16 or wider, within the bound.
A program may use at most 128 MiB of HBM per device.

v0:
```python
import jax
import jax.numpy as jnp
from jax import lax
from jax.sharding import PartitionSpec as P

CL_DEV = 384


epsilon = 1e-06
norm_floor = 0.25


def entering(part, axis, combine, identity):
    place = lax.axis_index(axis)
    gathered = lax.all_gather(part, axis)
    state = jnp.zeros_like(part) + jnp.asarray(identity, part.dtype)

    def one(hop, state):
        return combine(state, lax.dynamic_index_in_dim(gathered, hop, 0, False))

    return lax.fori_loop(0, place, one, state)


def shards(embeddings, cluster_ids, owner_bounds):
    groups = lax.axis_size("grp")
    replicas = lax.axis_size("rep")
    owner_total = groups * replicas
    position = lax.axis_index("grp") * replicas + lax.axis_index("rep")
    row_count = embeddings.shape[0]
    feature_count = embeddings.shape[1]
    clusters = CL_DEV * owner_total
    slot_count = 3 * row_count // owner_total
    owner_limit = CL_DEV + CL_DEV // 2
    row_range = jnp.arange(row_count, dtype=jnp.int32)
    owner_of = jnp.sum(owner_bounds[None, :] <= cluster_ids[:, None], axis=1, dtype=jnp.int32) - 1
    order = jnp.argsort(cluster_ids, stable=True)
    sorted_place = jnp.zeros((row_count,), jnp.int32).at[order].set(row_range)
    sorted_owner = owner_of[order]
    same_owner = sorted_place - jnp.searchsorted(sorted_owner, owner_of, side="left")
    target = owner_of * slot_count + same_owner
    counts = jnp.zeros((clusters,), jnp.int32).at[cluster_ids].add(1)
    before = entering(counts, ("grp", "rep"), jnp.add, jnp.zeros_like(counts))
    sorted_ids = cluster_ids[order]
    same_cluster = sorted_place - jnp.searchsorted(sorted_ids, cluster_ids, side="left")
    local_slot = before[cluster_ids] + same_cluster
    values = embeddings.astype(jnp.float32)
    unit_rows = (
        values * lax.rsqrt(jnp.sum(values * values, axis=1, keepdims=True) + epsilon)
    ).astype(jnp.bfloat16)
    send_rows = (
        jnp.zeros((owner_total * slot_count, feature_count), jnp.bfloat16).at[target].set(unit_rows)
    )
    send_ids = jnp.full((owner_total * slot_count,), -1, jnp.int32).at[target].set(cluster_ids)
    got_rows, got_ids = (
        lax.all_to_all(
            send_rows.reshape(owner_total, slot_count, feature_count),
            ("grp", "rep"),
            split_axis=0,
            concat_axis=0,
            tiled=True,
        ),
        lax.all_to_all(
            send_ids.reshape(owner_total, slot_count),
            ("grp", "rep"),
            split_axis=0,
            concat_axis=0,
            tiled=True,
        ),
    )
    flat_rows = got_rows.reshape(owner_total * slot_count, feature_count)
    flat_ids = got_ids.reshape(-1)
    local_index = flat_ids - owner_bounds[position]
    membership = jnp.arange(owner_limit)[:, None] == local_index[None, :]
    member_sums = jnp.dot(
        membership.astype(jnp.bfloat16), flat_rows, preferred_element_type=jnp.float32
    )
    members = jnp.sum(membership, axis=1, dtype=jnp.float32)
    centroid = member_sums / jnp.maximum(members, 1.0)[:, None]
    centroid_norm = jnp.sqrt(jnp.sum(centroid * centroid, axis=1))
    unit_centroid = (centroid / jnp.maximum(centroid_norm, norm_floor)[:, None]).astype(
        jnp.bfloat16
    )
    picked = unit_centroid[jnp.clip(local_index, 0, owner_limit - 1)]
    owner_distance = 1.0 - jnp.einsum(
        "rd,rd->r", flat_rows, picked, preferred_element_type=jnp.float32
    )
    returned = lax.all_to_all(
        owner_distance.reshape(owner_total, slot_count),
        ("grp", "rep"),
        split_axis=0,
        concat_axis=0,
        tiled=True,
    )
    distance = returned.reshape(-1)[target]
    return (distance, local_slot, unit_centroid[None])


def solution(mesh):
    placed = (P(("grp", "rep"), None), P(("grp", "rep")), P())
    return jax.shard_map(
        shards,
        mesh=mesh,
        in_specs=placed,
        out_specs=(P(("grp", "rep")), P(("grp", "rep")), P(("grp", "rep"), None, None)),
        check_vma=False,
    )
```

profile of v0, /device:TPU:0, one launch (start us, length us, event | category | flops | bytes accessed | tf_op | source)
XLA Modules:
  0.0 216.7 jit_solution(953403876074517466)
XLA Ops:
  7.2 0.0 all-gather.3.cloned.1.call-start
  7.2 0.7 compare_select_fusion.1
  7.9 3.8 %scatter_custom_fusion.3 = s32[12288]{0:T(1024)} fusion(s32[512]{0:T(512)S(1)} %compare_select_fusion.1, s32[512]{0:T(512)S(1)} %broadcast.93, s32[]{:T(128)} %constant.81.clone.1), kind=kCustom, calls=%fused_computation.37 | custom fusion | flops 512 | bytes 49156 | tf_op jit(solution)/shard_map/scatter-add | solution.py:41
  11.7 0.0 all-gather.3.cloned.1.call-update
  11.8 4.4 %sort.17 = (s32[512]{0:T(512)}, s32[512]{0:T(512)S(1)}) sort(s32[512]{0:T(512)} %param.10, s32[512]{0:T(512)S(1)} %iota.11), dimensions={0}, to_apply=%region_1.0 | sort | flops 4608 | bytes 8192 | tf_op jit(solution)/shard_map/jit(argsort)/sort | solution.py:36
  16.3 0.8 convert_reduce_fusion.1
  17.0 3.6 %gather_fusion.6 = s32[512]{0:T(512)S(1)} fusion(s32[512]{0:T(512)} %param.10, s32[1024]{0:T(1024)S(1)} %pad_clamp_fusion.5), kind=kCustom, calls=%fused_computation.6 | custom fusion | bytes 6144 | tf_op jit(solution)/shard_map/gather | solution.py:43
  20.7 3.5 %gather_fusion.2 = s32[512]{0:T(512)S(1)} fusion(s32[512]{0:T(512)S(1)} %broadcast_add_fusion, s32[1024]{0:T(1024)S(1)} %pad_clamp_fusion.5), kind=kCustom, calls=%fused_computation.2 | custom fusion | bytes 6144 | tf_op jit(solution)/shard_map/gather | solution.py:38
  24.2 0.0 copy-start
  24.2 35.9 %while.48 = (s32[]{:T(128)}, u32[512]{0:T(512)S(1)}, u32[512]{0:T(512)S(1)}, s32[512]{0:T(512)S(1)}, s32[512]{0:T(512)S(1)}, /*index=5*/s32[]{:T(128)}, s32[]{:T(128)}, s32[]{}) while((s32[]{:T(128)}, u32[512]{0:T(512)S(1)}, u32[512]{0:T(512)S(1)}, s32[512]{0:T(512)S(1)}, s32[512]{0:T(512)S(1)}, /*index=5*/s32[]{:T(128)}, ...), condition=%wide.region_4.5_spmd.clone, body=%wide.region_3.4_spmd.clone.sunk | while | flops 10244 | bytes 40045 | solution.py:39
  24.2 3.5 %gather_fusion = s32[512]{0:T(512)S(1)} fusion(s32[512]{0:T(512)S(1)} %get-tuple-element.385, u32[1024]{0:T(1024)S(1)} %pad_clamp_fusion.8), kind=kCustom, calls=%fused_computation.clone.clone.1 | custom fusion | bytes 6144 | tf_op jit(solution)/shard_map/jit(searchsorted)/jit(_searchsorted_scan_impl)/vmap(jit(_searchsorted_scan_impl))/while/body/eval_jaxpr/gather | solution.py:39
  27.8 3.5 %gather_fusion = s32[512]{0:T(512)S(1)} fusion(s32[512]{0:T(512)S(1)} %get-tuple-element.385, u32[1024]{0:T(1024)S(1)} %pad_clamp_fusion.8), kind=kCustom, calls=%fused_computation.clone.clone.1 | custom fusion | bytes 6144 | tf_op jit(solution)/shard_map/jit(searchsorted)/jit(_searchsorted_scan_impl)/vmap(jit(_searchsorted_scan_impl))/while/body/eval_jaxpr/gather | solution.py:39
  31.4 3.5 %gather_fusion = s32[512]{0:T(512)S(1)} fusion(s32[512]{0:T(512)S(1)} %get-tuple-element.385, u32[1024]{0:T(1024)S(1)} %pad_clamp_fusion.8), kind=kCustom, calls=%fused_computation.clone.clone.1 | custom fusion | bytes 6144 | tf_op jit(solution)/shard_map/jit(searchsorted)/jit(_searchsorted_scan_impl)/vmap(jit(_searchsorted_scan_impl))/while/body/eval_jaxpr/gather | solution.py:39
  35.0 3.5 %gather_fusion = s32[512]{0:T(512)S(1)} fusion(s32[512]{0:T(512)S(1)} %get-tuple-element.385, u32[1024]{0:T(1024)S(1)} %pad_clamp_fusion.8), kind=kCustom, calls=%fused_computation.clone.clone.1 | custom fusion | bytes 6144 | tf_op jit(solution)/shard_map/jit(searchsorted)/jit(_searchsorted_scan_impl)/vmap(jit(_searchsorted_scan_impl))/while/body/eval_jaxpr/gather | solution.py:39
  38.6 3.5 %gather_fusion = s32[512]{0:T(512)S(1)} fusion(s32[512]{0:T(512)S(1)} %get-tuple-element.385, u32[1024]{0:T(1024)S(1)} %pad_clamp_fusion.8), kind=kCustom, calls=%fused_computation.clone.clone.1 | custom fusion | bytes 6144 | tf_op jit(solution)/shard_map/jit(searchsorted)/jit(_searchsorted_scan_impl)/vmap(jit(_searchsorted_scan_impl))/while/body/eval_jaxpr/gather | solution.py:39
  42.2 3.5 %gather_fusion = s32[512]{0:T(512)S(1)} fusion(s32[512]{0:T(512)S(1)} %get-tuple-element.385, u32[1024]{0:T(1024)S(1)} %pad_clamp_fusion.8), kind=kCustom, calls=%fused_computation.clone.clone.1 | custom fusion | bytes 6144 | tf_op jit(solution)/shard_map/jit(searchsorted)/jit(_searchsorted_scan_impl)/vmap(jit(_searchsorted_scan_impl))/while/body/eval_jaxpr/gather | solution.py:39
  45.7 3.5 %gather_fusion = s32[512]{0:T(512)S(1)} fusion(s32[512]{0:T(512)S(1)} %get-tuple-element.385, u32[1024]{0:T(1024)S(1)} %pad_clamp_fusion.8), kind=kCustom, calls=%fused_computation.clone.clone.1 | custom fusion | bytes 6144 | tf_op jit(solution)/shard_map/jit(searchsorted)/jit(_searchsorted_scan_impl)/vmap(jit(_searchsorted_scan_impl))/while/body/eval_jaxpr/gather | solution.py:39
  49.3 3.5 %gather_fusion = s32[512]{0:T(512)S(1)} fusion(s32[512]{0:T(512)S(1)} %get-tuple-element.385, u32[1024]{0:T(1024)S(1)} %pad_clamp_fusion.8), kind=kCustom, calls=%fused_computation.clone.clone.1 | custom fusion | bytes 6144 | tf_op jit(solution)/shard_map/jit(searchsorted)/jit(_searchsorted_scan_impl)/vmap(jit(_searchsorted_scan_impl))/while/body/eval_jaxpr/gather | solution.py:39
  52.9 3.5 %gather_fusion = s32[512]{0:T(512)S(1)} fusion(s32[512]{0:T(512)S(1)} %get-tuple-element.385, u32[1024]{0:T(1024)S(1)} %pad_clamp_fusion.8), kind=kCustom, calls=%fused_computation.clone.clone.1 | custom fusion | bytes 6144 | tf_op jit(solution)/shard_map/jit(searchsorted)/jit(_searchsorted_scan_impl)/vmap(jit(_searchsorted_scan_impl))/while/body/eval_jaxpr/gather | solution.py:39
  56.5 3.5 %gather_fusion = s32[512]{0:T(512)S(1)} fusion(s32[512]{0:T(512)S(1)} %get-tuple-element.385, u32[1024]{0:T(1024)S(1)} %pad_clamp_fusion.8), kind=kCustom, calls=%fused_computation.clone.clone.1 | custom fusion | bytes 6144 | tf_op jit(solution)/shard_map/jit(searchsorted)/jit(_searchsorted_scan_impl)/vmap(jit(_searchsorted_scan_impl))/while/body/eval_jaxpr/gather | solution.py:39
  60.1 0.0 copy-done
  60.1 0.0 copy-start.3
  60.1 35.9 %while.49 = (s32[]{:T(128)}, u32[512]{0:T(512)S(1)}, u32[512]{0:T(512)S(1)}, s32[512]{0:T(512)S(1)}, s32[512]{0:T(512)S(1)}, /*index=5*/s32[]{:T(128)}, s32[]{:T(128)}, s32[]{}) while((s32[]{:T(128)}, u32[512]{0:T(512)S(1)}, u32[512]{0:T(512)S(1)}, s32[512]{0:T(512)S(1)}, s32[512]{0:T(512)S(1)}, /*index=5*/s32[]{:T(128)}, ...), condition=%wide.region_14.15_spmd.clone, body=%wide.region_13.14_spmd.clone.sunk | while | flops 10244 | bytes 40045 | solution.py:44
  60.1 3.5 %gather_fusion.1 = s32[512]{0:T(512)S(1)} fusion(s32[512]{0:T(512)S(1)} %get-tuple-element.361, u32[1024]{0:T(1024)S(1)} %pad_clamp_fusion.9), kind=kCustom, calls=%fused_computation.1.clone.clone.1 | custom fusion | bytes 6144 | tf_op jit(solution)/shard_map/jit(searchsorted)/jit(_searchsorted_scan_impl)/vmap(jit(_searchsorted_scan_impl))/while/body/eval_jaxpr/gather | solution.py:39
  63.7 3.5 %gather_fusion.1 = s32[512]{0:T(512)S(1)} fusion(s32[512]{0:T(512)S(1)} %get-tuple-element.361, u32[1024]{0:T(1024)S(1)} %pad_clamp_fusion.9), kind=kCustom, calls=%fused_computation.1.clone.clone.1 | custom fusion | bytes 6144 | tf_op jit(solution)/shard_map/jit(searchsorted)/jit(_searchsorted_scan_impl)/vmap(jit(_searchsorted_scan_impl))/while/body/eval_jaxpr/gather | solution.py:39
  67.3 3.5 %gather_fusion.1 = s32[512]{0:T(512)S(1)} fusion(s32[512]{0:T(512)S(1)} %get-tuple-element.361, u32[1024]{0:T(1024)S(1)} %pad_clamp_fusion.9), kind=kCustom, calls=%fused_computation.1.clone.clone.1 | custom fusion | bytes 6144 | tf_op jit(solution)/shard_map/jit(searchsorted)/jit(_searchsorted_scan_impl)/vmap(jit(_searchsorted_scan_impl))/while/body/eval_jaxpr/gather | solution.py:39
  70.9 3.5 %gather_fusion.1 = s32[512]{0:T(512)S(1)} fusion(s32[512]{0:T(512)S(1)} %get-tuple-element.361, u32[1024]{0:T(1024)S(1)} %pad_clamp_fusion.9), kind=kCustom, calls=%fused_computation.1.clone.clone.1 | custom fusion | bytes 6144 | tf_op jit(solution)/shard_map/jit(searchsorted)/jit(_searchsorted_scan_impl)/vmap(jit(_searchsorted_scan_impl))/while/body/eval_jaxpr/gather | solution.py:39
  74.5 3.5 %gather_fusion.1 = s32[512]{0:T(512)S(1)} fusion(s32[512]{0:T(512)S(1)} %get-tuple-element.361, u32[1024]{0:T(1024)S(1)} %pad_clamp_fusion.9), kind=kCustom, calls=%fused_computation.1.clone.clone.1 | custom fusion | bytes 6144 | tf_op jit(solution)/shard_map/jit(searchsorted)/jit(_searchsorted_scan_impl)/vmap(jit(_searchsorted_scan_impl))/while/body/eval_jaxpr/gather | solution.py:39
  78.1 3.5 %gather_fusion.1 = s32[512]{0:T(512)S(1)} fusion(s32[512]{0:T(512)S(1)} %get-tuple-element.361, u32[1024]{0:T(1024)S(1)} %pad_clamp_fusion.9), kind=kCustom, calls=%fused_computation.1.clone.clone.1 | custom fusion | bytes 6144 | tf_op jit(solution)/shard_map/jit(searchsorted)/jit(_searchsorted_scan_impl)/vmap(jit(_searchsorted_scan_impl))/while/body/eval_jaxpr/gather | solution.py:39
  81.7 3.5 %gather_fusion.1 = s32[512]{0:T(512)S(1)} fusion(s32[512]{0:T(512)S(1)} %get-tuple-element.361, u32[1024]{0:T(1024)S(1)} %pad_clamp_fusion.9), kind=kCustom, calls=%fused_computation.1.clone.clone.1 | custom fusion | bytes 6144 | tf_op jit(solution)/shard_map/jit(searchsorted)/jit(_searchsorted_scan_impl)/vmap(jit(_searchsorted_scan_impl))/while/body/eval_jaxpr/gather | solution.py:39
  85.2 3.5 %gather_fusion.1 = s32[512]{0:T(512)S(1)} fusion(s32[512]{0:T(512)S(1)} %get-tuple-element.361, u32[1024]{0:T(1024)S(1)} %pad_clamp_fusion.9), kind=kCustom, calls=%fused_computation.1.clone.clone.1 | custom fusion | bytes 6144 | tf_op jit(solution)/shard_map/jit(searchsorted)/jit(_searchsorted_scan_impl)/vmap(jit(_searchsorted_scan_impl))/while/body/eval_jaxpr/gather | solution.py:39
  88.8 3.5 %gather_fusion.1 = s32[512]{0:T(512)S(1)} fusion(s32[512]{0:T(512)S(1)} %get-tuple-element.361, u32[1024]{0:T(1024)S(1)} %pad_clamp_fusion.9), kind=kCustom, calls=%fused_computation.1.clone.clone.1 | custom fusion | bytes 6144 | tf_op jit(solution)/shard_map/jit(searchsorted)/jit(_searchsorted_scan_impl)/vmap(jit(_searchsorted_scan_impl))/while/body/eval_jaxpr/gather | solution.py:39
  92.4 3.5 %gather_fusion.1 = s32[512]{0:T(512)S(1)} fusion(s32[512]{0:T(512)S(1)} %get-tuple-element.361, u32[1024]{0:T(1024)S(1)} %pad_clamp_fusion.9), kind=kCustom, calls=%fused_computation.1.clone.clone.1 | custom fusion | bytes 6144 | tf_op jit(solution)/shard_map/jit(searchsorted)/jit(_searchsorted_scan_impl)/vmap(jit(_searchsorted_scan_impl))/while/body/eval_jaxpr/gather | solution.py:39
  96.0 2.4 %scatter_custom_fusion = s32[512]{0:T(512)S(1)} fusion(s32[512]{0:T(512)S(1)} %compare_select_fusion.3, s32[512]{0:T(512)S(1)} %iota.12, s32[]{:T(128)} %constant.81.clone.1), kind=kCustom, calls=%fused_computation.56 | custom fusion | bytes 2052 | tf_op jit(solution)/shard_map/scatter | solution.py:37
  98.5 0.2 fusion.3
  98.7 0.0 all-gather.3.cloned.1.call-done
  98.7 1.6 reshape.167
  100.4 3.1 %gather_fusion.5 = s32[512]{0:T(512)S(1)} fusion(s32[12288]{0:T(1024)S(1)} %get-tuple-element.149, s32[1024]{0:T(1024)S(1)} %pad_clamp_fusion.3), kind=kCustom, calls=%fused_computation.5 | custom fusion | bytes 6144 | tf_op jit(solution)/shard_map/gather | solution.py:45
  103.5 0.6 subtract_add_fusion
  104.1 2.4 %scatter_custom_fusion.2 = s32[1536]{0:T(1024)S(1)} fusion(s32[512]{0:T(512)S(1)} %get-tuple-element.222, s32[512]{0:T(512)S(1)} %get-tuple-element.391, s32[]{:T(128)} %constant.82.clone.1), kind=kCustom, calls=%fused_computation.50 | custom fusion | bytes 6148 | tf_op jit(solution)/shard_map/scatter | solution.py:53
  106.6 0.7 all_to_all.16
  107.3 9.6 %all-to-all-start.1 = ((s32[32,1,48]{2,1,0:T(1,128)}), s32[32,1,48]{2,1,0:T(1,128)S(1)}, u32[]{:S(2)}, u32[]{:S(2)}) async-start(s32[32,1,48]{2,1,0:T(1,128)} %all_to_all.16), calls=%async_computation.1 | async-start | bytes 32768 | tf_op jit(solution)/shard_map/all_to_all | solution.py:62
  116.9 4.4 %scatter_custom_fusion.1 = bf16[1536,768]{1,0:T(8,128)(2,1)} fusion(s32[512]{0:T(512)S(1)} %get-tuple-element.222, bf16[]{:T(256)} %constant.80.clone.1, bf16[512,768]{1,0:T(8,128)(2,1)S(1)} %copy-done.3, f32[512]{0:T(512)S(1)} %add_rsqrt_fusion), kind=kCustom, calls=%fused_computation.32 | custom fusion | flops 1179648 | bytes 3147778 | tf_op jit(solution)/shard_map/scatter | solution.py:51
  121.3 2.7 %all-to-all-done.1 = s32[32,1,48]{2,1,0:T(1,128)S(1)} async-done(((s32[32,1,48]{2,1,0:T(1,128)}), s32[32,1,48]{2,1,0:T(1,128)S(1)}, u32[]{:S(2)}, u32[]{:S(2)}) %all-to-all-start.1) | async-done | bytes 6176 | tf_op jit(solution)/shard_map/all_to_all | solution.py:62
  124.0 3.3 %all-to-all-start = ((bf16[32,48,768]{2,1,0:T(8,128)(2,1)}), bf16[32,48,768]{2,1,0:T(8,128)(2,1)S(1)}, u32[]{:S(2)}, u32[]{:S(2)}) async-start(bf16[32,48,768]{2,1,0:T(8,128)(2,1)} %bitcast.11), calls=%async_computation | async-start | bytes 4718592 | tf_op jit(solution)/shard_map/all_to_all | solution.py:55
  127.3 0.6 dynamic_slice.7
  127.9 0.7 clamp_reduce_fusion
  128.7 0.1 sub.56
  128.7 0.1 min.12
  128.9 0.4 convert_reduce_fusion
  129.3 53.4 %all-to-all-done = bf16[32,48,768]{2,1,0:T(8,128)(2,1)S(1)} async-done(((bf16[32,48,768]{2,1,0:T(8,128)(2,1)}), bf16[32,48,768]{2,1,0:T(8,128)(2,1)S(1)}, u32[]{:S(2)}, u32[]{:S(2)}) %all-to-all-start) | async-done | bytes 2359328 | tf_op jit(solution)/shard_map/all_to_all | solution.py:55
  182.7 1.8 multiply_reduce_fusion
  184.5 1.2 copy-done.2
  185.7 0.2 divide_convert_fusion
  185.9 5.0 %gather_fusion.3 = bf16[1536,768]{1,0:T(8,128)(2,1)S(1)} fusion(bf16[576,768]{1,0:T(8,128)(2,1)S(1)} %divide_convert_fusion, s32[2048]{0:T(1024)S(1)} %pad_clamp_fusion.2), kind=kCustom, calls=%fused_computation.3 | custom fusion | bytes 4724736 | tf_op jit(solution)/shard_map/gather | solution.py:83
  190.9 2.5 %fusion = f32[1536]{0:T(1024)S(1)} fusion(bf16[1536,768]{1,0:T(8,128)(2,1)S(1)} %gather_fusion.3, bf16[32,48,768]{2,1,0:T(8,128)(2,1)} %copy-done.1), kind=kLoop, calls=%fused_computation.21 | loop fusion | flops 4717056 | bytes 4724736 | tf_op jit(solution)/shard_map/rd,rd->r/dot_general | solution.py:84
  193.3 0.7 all_to_all.18
  194.0 3.1 %all-to-all-start.2 = ((f32[32,1,48]{2,1,0:T(1,128)}), f32[32,1,48]{2,1,0:T(1,128)S(1)}, u32[]{:S(2)}, u32[]{:S(2)}) async-start(f32[32,1,48]{2,1,0:T(1,128)} %all_to_all.18), calls=%async_computation.2 | async-start | bytes 32768 | tf_op jit(solution)/shard_map/all_to_all | solution.py:87
  197.2 2.6 %fusion.17 = bf16[1,576,768]{2,1,0:T(8,128)(2,1)} fusion(f32[576,768]{1,0:T(8,128)} %copy-done.2, f32[576]{0:T(1024)S(1)} %maximum_multiply_fusion), kind=kLoop, calls=%fused_computation.59 | loop fusion | flops 884736 | bytes 2656512 | tf_op jit(solution)/shard_map/broadcast_in_dim | solution.py:95
  199.7 4.6 %all-to-all-done.2 = f32[32,1,48]{2,1,0:T(1,128)S(1)} async-done(((f32[32,1,48]{2,1,0:T(1,128)}), f32[32,1,48]{2,1,0:T(1,128)S(1)}, u32[]{:S(2)}, u32[]{:S(2)}) %all-to-all-start.2) | async-done | bytes 6176 | tf_op jit(solution)/shard_map/all_to_all | solution.py:87
  204.3 0.5 broadcast.197
  204.8 0.7 reduce.15
  205.5 0.1 reshape.78
  205.6 4.3 %gather_fusion.4 = f32[512]{0:T(512)} fusion(f32[1536]{0:T(1024)S(1)} %reshape.78, s32[1024]{0:T(1024)S(1)} %pad_clamp_fusion.4), kind=kCustom, calls=%fused_computation.4 | custom fusion | bytes 6144 | tf_op jit(solution)/shard_map/gather | solution.py:94
  (126 shorter events, 1.0 us)
Async XLA Ops:
  7.2 91.6 %all-gather.3.cloned.1.call-start = ((), (), s32[]{:S(2)}) async-start(), calls=%async_computation.3 | async-start | bytes 1622016 | tf_op jit(solution)/shard_map/all_gather | solution.py:15
  24.2 35.9 %copy-start = (s32[512]{0:T(512)S(1)}, s32[512]{0:T(512)}, u32[]{:S(2)}) copy-start(s32[512]{0:T(512)} %param.10) | copy-start | bytes 6148
  60.1 38.4 %copy-start.3 = (bf16[512,768]{1,0:T(8,128)(2,1)S(1)}, bf16[512,768]{1,0:T(8,128)(2,1)}, u32[]{:S(2)}) copy-start(bf16[512,768]{1,0:T(8,128)(2,1)} %param.9) | copy-start | bytes 2359300
  107.3 16.7 %all-to-all-start.1 = ((s32[32,1,48]{2,1,0:T(1,128)}), s32[32,1,48]{2,1,0:T(1,128)S(1)}, u32[]{:S(2)}, u32[]{:S(2)}) async-start(s32[32,1,48]{2,1,0:T(1,128)} %all_to_all.16), calls=%async_computation.1 | async-start | bytes 32768 | tf_op jit(solution)/shard_map/all_to_all | solution.py:62
  124.0 3.3 %copy-start.4 = (s32[32]{0:T(128)S(1)}, s32[32]{0:T(128)}, u32[]{:S(2)}) copy-start(s32[32]{0:T(128)} %param.11) | copy-start | bytes 388
  124.0 58.8 %all-to-all-start = ((bf16[32,48,768]{2,1,0:T(8,128)(2,1)}), bf16[32,48,768]{2,1,0:T(8,128)(2,1)S(1)}, u32[]{:S(2)}, u32[]{:S(2)}) async-start(bf16[32,48,768]{2,1,0:T(8,128)(2,1)} %bitcast.11), calls=%async_computation | async-start | bytes 4718592 | tf_op jit(solution)/shard_map/all_to_all | solution.py:55
  182.7 1.8 copy-start.1
  184.5 1.2 copy-start.2
  194.0 10.3 %all-to-all-start.2 = ((f32[32,1,48]{2,1,0:T(1,128)}), f32[32,1,48]{2,1,0:T(1,128)S(1)}, u32[]{:S(2)}, u32[]{:S(2)}) async-start(f32[32,1,48]{2,1,0:T(1,128)} %all_to_all.18), calls=%async_computation.2 | async-start | bytes 32768 | tf_op jit(solution)/shard_map/all_to_all | solution.py:87
Sparse Core Ops, SparseCore 0:
  11.9 57.7 all-gather.2
where the time goes:
time: 217 us
  local copies, waits for them, and re-layouts  99.8 us (46%)
  waiting for transfers between devices  60.7 us (28%)
  other arithmetic  22.9 us (11%)
  starting transfers between devices  16.1 us (7%)
  between operations  14.3 us (7%)
    gather x20, local copies, waits for them, and re-layouts, shards(): jnp.searchsorted(sorted_owner, owner_of, side='left')  69.8 us
    all_to_all x1, waiting for transfers between devices, shards(): lax.all_to_all(send_rows.reshape(owner_total, slot_count, feature_count),...  53.4 us
    all_to_all x1, starting transfers between devices, shards(): lax.all_to_all(send_ids.reshape(owner_total, slot_count), ('grp', 'rep'),...  9.63 us
    gather x1, local copies, waits for them, and re-layouts, shards(): picked = unit_centroid[jnp.clip(local_index, 0, owner_limit - 1)]  4.97 us
    all_to_all x1, waiting for transfers between devices, shards(): lax.all_to_all(owner_distance.reshape(owner_total, slot_count), ('grp', '...  4.57 us
    sort x1, other arithmetic, shards(): order = jnp.argsort(cluster_ids, stable=True)  4.45 us
    scatter x1, other arithmetic, shards(): jnp.zeros((owner_total * slot_count, feature_count), jnp.bfloat16)  4.36 us
  transfers between devices with their start and end apart: 4, of which 3 were waited for; matrix products, arithmetic and copies ran while one was open for 44% of the time, Pallas kernels for 0%

commit v1 on v0

v1 whole, which is shorter than its diff:
```python
import functools

import jax
import jax.numpy as jnp
from jax import lax
from jax.experimental import pallas as pl
from jax.experimental.pallas import tpu as pltpu
from jax.sharding import PartitionSpec as P

CL_DEV = 384
LANES = 128

epsilon = 1e-06
norm_floor = 0.25
MESH = pl.DeviceIdType.MESH
F32 = jnp.float32
BF16 = jnp.bfloat16
EXACT = lax.Precision.HIGHEST
NT = (((1,), (1,)), ((), ()))


def iota(shape, dim):
    return lax.broadcasted_iota(jnp.int32, shape, dim)


def ones_at(mask, kind):
    return jnp.where(mask, 1.0, 0.0).astype(kind)


def digits_dot(table, place):
    high = jnp.floor(table * (1.0 / 32.0))
    low = table - 32.0 * high
    upper = jnp.dot(high.astype(BF16), place, preferred_element_type=F32)
    lower = jnp.dot(low.astype(BF16), place, preferred_element_type=F32)
    return 32.0 * upper + lower


def kernel(
    groups, replicas, slots,
    emb_ref, ids_ref, bounds_ref,
    cent_ref, dist_ref, rank_ref,
    unit, send_rows, got_rows, send_ids, got_ids, member, total, ret, got_ret, slot_mat,
    row_send, row_recv, id_send, id_recv, ret_send, ret_recv,
):
    my_group = lax.axis_index("grp")
    my_replica = lax.axis_index("rep")
    me = my_group * replicas + my_replica
    owners = groups * replicas
    rows, width = emb_ref.shape
    limit = cent_ref.shape[0]
    block = replicas * slots

    def peer(dg, dr):
        return lax.rem(my_group + dg, groups), lax.rem(my_replica + dr, replicas)

    def source(dg, dr):
        return (
            lax.rem(my_group + groups - dg, groups),
            lax.rem(my_replica + replicas - dr, replicas),
        )

    def every(dg, act):
        def one(dr, carry):
            act(dr)
            return carry

        lax.fori_loop(1 if dg == 0 else 0, replicas, one, 0)

    def copy(src, dst, ssem, rsem, pair, here, there):
        return pltpu.make_async_remote_copy(
            src_ref=src.at[there],
            dst_ref=dst.at[here],
            send_sem=ssem.at[there],
            recv_sem=rsem.at[here],
            device_id=pair,
            device_id_type=MESH,
        )

    def start(bufs, dg, dr):
        pair = peer(dg, dr)
        copy(*bufs, pair, me, pair[0] * replicas + pair[1]).start()

    def wait_send(bufs, dg, dr):
        pair = peer(dg, dr)
        copy(*bufs, pair, me, pair[0] * replicas + pair[1]).wait_send()

    def wait_recv(bufs, dg, dr):
        pair = source(dg, dr)
        there = pair[0] * replicas + pair[1]
        copy(*bufs, pair, there, there).wait_recv()

    row_bufs = (send_rows, got_rows, row_send, row_recv)
    id_bufs = (send_ids, got_ids, id_send, id_recv)
    ret_bufs = (ret, got_ret, ret_send, ret_recv)
    order = list(range(1, groups)) + [0]

    barrier = pltpu.get_barrier_semaphore()
    for dg in order:
        every(
            dg,
            lambda dr, dg=dg: pl.semaphore_signal(
                barrier, inc=1, device_id=peer(dg, dr), device_id_type=MESH
            ),
        )

    ids = ids_ref[...]
    edges = bounds_ref[...]
    reached = ones_at(edges <= ids, F32)
    owner = jnp.sum(reached, axis=0, keepdims=True).astype(jnp.int32) - 1
    owned = iota((owners, rows), 0) == owner
    owned_f = ones_at(owned, F32)
    first = jnp.sum(owned_f * edges.astype(F32), axis=0, keepdims=True)
    local = ids.astype(F32) - first
    earlier = ones_at(iota((rows, rows), 0) < iota((rows, rows), 1), BF16)
    prefix = jnp.dot(owned_f.astype(BF16), earlier, preferred_element_type=F32)
    rank = jnp.sum(owned_f * prefix, axis=0, keepdims=True).astype(jnp.int32)
    target = owner * slots + rank
    place = ones_at(iota((LANES, rows), 0) == rank, BF16)
    high = jnp.floor(local * (1.0 / 32.0))
    low = local - 32.0 * high
    upper = lax.dot_general((owned_f * high).astype(BF16), place, NT, preferred_element_type=F32)
    lower = lax.dot_general((owned_f * low).astype(BF16), place, NT, preferred_element_type=F32)
    filled = lax.dot_general(owned_f.astype(BF16), place, NT, preferred_element_type=F32)
    id_table = 32.0 * upper + lower + filled - 1.0
    for o in range(owners):
        send_ids[o] = jnp.broadcast_to(id_table[o : o + 1, :], (8, LANES))
    got_ids[me] = send_ids[me]

    values = emb_ref[...].astype(F32)
    unit[...] = (
        values * lax.rsqrt(jnp.sum(values * values, axis=1, keepdims=True) + epsilon)
    ).astype(BF16)

    pl.semaphore_wait(barrier, owners - 1)
    for dg in order:
        every(dg, lambda dr, dg=dg: start(id_bufs, dg, dr))
    for dg in order:
        tg = lax.rem(my_group + dg, groups)
        pick = ones_at(iota((block, rows), 0) + tg * block == target, BF16)
        packed = jnp.dot(pick, unit[...], preferred_element_type=F32).astype(BF16)
        send_rows[pl.ds(tg * replicas, replicas)] = packed.reshape(replicas, slots, width)
        every(dg, lambda dr, dg=dg: start(row_bufs, dg, dr))
    got_rows[me] = send_rows[me]

    for dg in order:
        every(dg, lambda dr, dg=dg: wait_recv(id_bufs, dg, dr))

    lane = iota((1, block), 1)
    quotient = jnp.zeros((1, block), jnp.int32)
    for s in range(1, replicas):
        quotient = quotient + jnp.where(lane >= s * slots, 1, 0)
    remainder = lane - quotient * slots
    spread = iota((LANES, block), 0) == remainder
    spread_b, spread_f = ones_at(spread, BF16), ones_at(spread, F32)
    from_source = ones_at(iota((replicas, block), 0) == quotient, F32)
    before = ones_at(iota((block, block), 0) < iota((block, block), 1), BF16)
    cluster = iota((limit, block), 0)

    seen = jnp.zeros((limit, 1), F32)
    for sg in range(groups):
        table = got_ids[sg * replicas : (sg + 1) * replicas, 0, :]
        flat = jnp.sum(from_source * digits_dot(table, spread_b), axis=0, keepdims=True)
        mask = ones_at(cluster == flat.astype(jnp.int32), F32)
        mask_b = mask.astype(BF16)
        member[sg] = mask_b
        ahead = jnp.dot(mask_b, before, preferred_element_type=F32) + seen
        slot = jnp.sum(mask * ahead, axis=0, keepdims=True)
        seen = seen + jnp.sum(mask, axis=1, keepdims=True)
        slot_mat[sg] = lax.dot_general(
            from_source * slot, spread_f, NT, precision=EXACT, preferred_element_type=F32
        )
    total[...] = jnp.zeros_like(total)
    for dg in order:
        sg = lax.rem(my_group + groups - dg, groups)
        every(dg, lambda dr, dg=dg: wait_recv(row_bufs, dg, dr))
        block_rows = got_rows[pl.ds(sg * replicas, replicas)].reshape(block, width)
        total[...] += jnp.dot(member[sg], block_rows, preferred_element_type=F32)

    centroid = total[...] / jnp.maximum(seen, 1.0)
    norm = jnp.sqrt(jnp.sum(centroid * centroid, axis=1, keepdims=True))
    cent_ref[...] = (centroid / jnp.maximum(norm, norm_floor)).astype(BF16)

    for dg in order:
        sg = lax.rem(my_group + groups - dg, groups)
        tg = lax.rem(my_group + groups - dg, groups)
        block_rows = got_rows[pl.ds(sg * replicas, replicas)].reshape(block, width)
        score = lax.dot_general(cent_ref[...], block_rows, NT, preferred_element_type=F32)
        near = jnp.sum(member[sg].astype(F32) * score, axis=0, keepdims=True)
        dist_mat = lax.dot_general(
            from_source * (1.0 - near), spread_f, NT, precision=EXACT, preferred_element_type=F32
        )
        rank_mat = slot_mat[sg]
        top = iota((8, LANES), 0) == 0
        for s in range(replicas):
            ret[tg * replicas + s] = jnp.where(top, dist_mat[s : s + 1, :], rank_mat[s : s + 1, :])
        back = (groups - dg) % groups
        every(back, lambda dr, back=back: start(ret_bufs, back, dr))
    got_ret[me] = ret[me]

    place_f = ones_at(iota((LANES, rows), 0) == rank, F32)
    for dg in order:
        every(dg, lambda dr, dg=dg: wait_recv(ret_bufs, dg, dr))
    dist_all = jnp.dot(got_ret[:, 0, :], place_f, precision=EXACT, preferred_element_type=F32)
    rank_all = jnp.dot(got_ret[:, 1, :], place_f, precision=EXACT, preferred_element_type=F32)
    dist_ref[...] = jnp.sum(owned_f * dist_all, axis=0, keepdims=True)
    rank_ref[...] = jnp.sum(owned_f * rank_all, axis=0, keepdims=True).astype(jnp.int32)
    for bufs in (id_bufs, row_bufs, ret_bufs):
        for dg in order:
            every(dg, lambda dr, dg=dg, bufs=bufs: wait_send(bufs, dg, dr))


def solution(mesh):
    groups, replicas = mesh.shape["grp"], mesh.shape["rep"]
    owners = groups * replicas

    def shards(embeddings, cluster_ids, owner_bounds):
        rows, width = embeddings.shape
        limit = CL_DEV + CL_DEV // 2
        slots = -(-(3 * rows // owners) // 16) * 16
        block = replicas * slots
        vmem = pl.BlockSpec(memory_space=pltpu.VMEM)
        small = pltpu.VMEM((owners, 8, LANES), F32)
        dma = pltpu.SemaphoreType.DMA((owners,))
        centroids, distance, rank = pl.pallas_call(
            functools.partial(kernel, groups, replicas, slots),
            out_shape=(
                jax.ShapeDtypeStruct((limit, width), BF16),
                jax.ShapeDtypeStruct((1, rows), F32),
                jax.ShapeDtypeStruct((1, rows), jnp.int32),
            ),
            in_specs=[vmem] * 3,
            out_specs=(vmem,) * 3,
            scratch_shapes=[
                pltpu.VMEM((rows, width), BF16),
                pltpu.VMEM((owners, slots, width), BF16),
                pltpu.VMEM((owners, slots, width), BF16),
                small,
                small,
                pltpu.VMEM((groups, limit, block), BF16),
                pltpu.VMEM((limit, width), F32),
                small,
                small,
                pltpu.VMEM((groups, replicas, LANES), F32),
                dma, dma, dma, dma, dma, dma,
            ],
            compiler_params=pltpu.CompilerParams(
                collective_id=0, has_side_effects=True, vmem_limit_bytes=56 * 1024 * 1024
            ),
        )(embeddings, cluster_ids.reshape(1, rows), owner_bounds.reshape(owners, 1))
        return distance.reshape(rows), rank.reshape(rows), centroids[None]

    placed = (P(("grp", "rep"), None), P(("grp", "rep")), P())
    return jax.shard_map(
        shards,
        mesh=mesh,
        in_specs=placed,
        out_specs=(P(("grp", "rep")), P(("grp", "rep")), P(("grp", "rep"), None, None)),
        check_vma=False,
    )
```

time: 217 us -> 84 us (0.39)
  local copies, waits for them, and re-layouts: 99.8 us -> 5.36 us
  Pallas kernels: 0 us -> 77.7 us
  waiting for transfers between devices: 60.7 us -> 0 us
  other arithmetic: 22.9 us -> 0 us
  starting transfers between devices: 16.1 us -> 0 us
  between operations: 14.3 us -> 0.66 us
    gather x25 -> x0, local copies, waits for them, and re-layouts: 89.3 us -> none  [the longest x20 69.8 us: shards(): jnp.searchsorted(sorted_owner, owner_of, side='left')]
    pallas_call x0 -> x1, Pallas kernels: none -> 77.7 us  [shards(): pl.pallas_call(functools.partial(kernel, groups, replicas, slots), out_sh...]
    all_to_all x3 -> x0, waiting for transfers between devices: 60.7 us -> none  [the longest x1 53.4 us: shards(): lax.all_to_all(send_rows.reshape(owner_total, slot_count, feature_count),...]
    all_to_all x3 -> x0, starting transfers between devices: 16.1 us -> none  [the longest x1 9.63 us: shards(): lax.all_to_all(send_ids.reshape(owner_total, slot_count), ('grp', 'rep'),...]
    scatter x2 -> x0, local copies, waits for them, and re-layouts: 4.88 us -> none  [the longest x1 2.45 us: shards(): jnp.full((owner_total * slot_count,), -1, jnp.int32).at[target]]
    sort x1 -> x0, other arithmetic: 4.45 us -> none  [shards(): order = jnp.argsort(cluster_ids, stable=True)]
    scatter x1 -> x0, other arithmetic: 4.36 us -> none  [shards(): jnp.zeros((owner_total * slot_count, feature_count), jnp.bfloat16)]
    scatter-add x1 -> x0, other arithmetic: 3.83 us -> none  [shards(): counts = jnp.zeros((clusters,), jnp.int32).at[cluster_ids].add(1)]
  transfers between devices with their start and end apart: 4 -> 0, of which waited for: 3 -> 0; matrix products, arithmetic and copies ran while one was open for 44% -> 0% of each run, Pallas kernels for 0% -> 0%
where the time goes in v1:
time: 84 us; the launch traced here: 83.7 us
  Pallas kernels  77.7 us (92%)
  local copies, waits for them, and re-layouts  5.36 us (6%)
    pallas_call x1, Pallas kernels, shards(): pl.pallas_call(functools.partial(kernel, groups, replicas, slots), out_sh...  77.7 us
    unnamed x9, local copies, waits for them, and re-layouts  4.67 us

profile of v1, /device:TPU:0, one launch (start us, length us, event | category | flops | bytes accessed | tf_op | source)
XLA Modules:
  0.0 83.7 jit_solution(1914156948841041846)
XLA Ops:
  0.6 0.0 copy-start.2
  0.6 0.6 copy-done.2
  1.3 0.7 copy.6.bounds_ref
  2.0 77.7 %shard_map.58 = (bf16[576,768]{1,0:T(8,128)(2,1)}, f32[1,512]{1,0:T(1,128)}, s32[1,512]{1,0:T(1,128)}) custom-call(bf16[512,768]{1,0:T(8,128)(2,1)} %emb_ref.1, s32[1,512]{1,0:T(1,128)} %bitcast.6, s32[32,1]{1,0:T(8,128)} %copy.6.bounds_ref), custom_call_target="tpu_custom_call" | custom-call | tf_op jit(solution)/shard_map/pallas_call | solution.py:224
  79.7 0.0 copy-start.1
  79.7 0.7 copy-done.1
  80.4 0.0 copy-start
  80.4 0.6 copy.10
  80.9 0.1 copy-done
  81.0 0.6 copy.11
  81.6 2.1 %copy.12 = bf16[1,576,768]{2,1,0:T(8,128)(2,1)} copy(bf16[1,576,768]{2,1,0:T(8,128)(2,1)} %bitcast.5) | data formatting | bytes 1769472
Async XLA Ops:
  0.6 0.7 copy-start.2
  79.7 0.7 copy-start.1
  80.4 0.7 copy-start

commit v2 on v1

--- a/solution.py
+++ b/solution.py
@@ -36,11 +36,12 @@
 
 
 def kernel(
-    groups, replicas, slots,
+    groups, replicas, direct, extra,
     emb_ref, ids_ref, bounds_ref,
-    cent_ref, dist_ref, rank_ref,
+    cent_ref, dist_ref, rank_ref, over_ref,
     unit, send_rows, got_rows, send_ids, got_ids, member, total, ret, got_ret, slot_mat,
     row_send, row_recv, id_send, id_recv, ret_send, ret_recv,
+    near_send, near_recv, far_send, far_recv,
 ):
     my_group = lax.axis_index("grp")
     my_replica = lax.axis_index("rep")
@@ -48,7 +49,9 @@
     owners = groups * replicas
     rows, width = emb_ref.shape
     limit = cent_ref.shape[0]
+    slots = direct + extra
     block = replicas * slots
+    sent = replicas * direct
 
     def peer(dg, dr):
         return lax.rem(my_group + dg, groups), lax.rem(my_replica + dr, replicas)
@@ -69,7 +72,7 @@
     def copy(src, dst, ssem, rsem, pair, here, there):
         return pltpu.make_async_remote_copy(
             src_ref=src.at[there],
-            dst_ref=dst.at[here],
+            dst_ref=dst.at[here, pl.ds(0, direct)] if dst is got_rows else dst.at[here],
             send_sem=ssem.at[there],
             recv_sem=rsem.at[here],
             device_id=pair,
@@ -114,36 +117,97 @@
     earlier = ones_at(iota((rows, rows), 0) < iota((rows, rows), 1), BF16)
     prefix = jnp.dot(owned_f.astype(BF16), earlier, preferred_element_type=F32)
     rank = jnp.sum(owned_f * prefix, axis=0, keepdims=True).astype(jnp.int32)
-    target = owner * slots + rank
-    place = ones_at(iota((LANES, rows), 0) == rank, BF16)
-    high = jnp.floor(local * (1.0 / 32.0))
-    low = local - 32.0 * high
-    upper = lax.dot_general((owned_f * high).astype(BF16), place, NT, preferred_element_type=F32)
-    lower = lax.dot_general((owned_f * low).astype(BF16), place, NT, preferred_element_type=F32)
-    filled = lax.dot_general(owned_f.astype(BF16), place, NT, preferred_element_type=F32)
-    id_table = 32.0 * upper + lower + filled - 1.0
-    for o in range(owners):
-        send_ids[o] = jnp.broadcast_to(id_table[o : o + 1, :], (8, LANES))
-    got_ids[me] = send_ids[me]
+    target = jnp.where(rank < direct, owner * direct + rank, -1)
+    spot = rank
+    if extra:
+        late = ones_at(rank >= direct, F32)
+        queue = jnp.dot(
+            jnp.broadcast_to(late, (8, rows)).astype(BF16), earlier, preferred_element_type=F32
+        )[0:1, :].astype(jnp.int32)
+        spot = jnp.where(rank < direct, rank, direct + queue)
+    place = ones_at(iota((LANES, rows), 0) == spot, BF16)
 
     values = emb_ref[...].astype(F32)
     unit[...] = (
         values * lax.rsqrt(jnp.sum(values * values, axis=1, keepdims=True) + epsilon)
     ).astype(BF16)
 
+    def pack(dg):
+        tg = lax.rem(my_group + dg, groups)
+        pick = ones_at(iota((sent, rows), 0) + tg * sent == target, BF16)
+        packed = jnp.dot(pick, unit[...], preferred_element_type=F32).astype(BF16)
+        send_rows[pl.ds(tg * replicas, replicas)] = packed.reshape(replicas, direct, width)
+
+    def near_copy(pair, owner_at, dr):
+        ref = got_rows.at[owner_at, pl.ds(direct, extra)]
+        return pltpu.make_async_remote_copy(
+            src_ref=ref, dst_ref=ref, send_sem=near_send.at[dr], recv_sem=near_recv.at[dr],
+            device_id=pair, device_id_type=MESH,
+        )
+
+    def far_copy(group_at, to_group, dg):
+        ref = got_rows.at[pl.ds(group_at * replicas, replicas), pl.ds(direct, extra)]
+        return pltpu.make_async_remote_copy(
+            src_ref=ref, dst_ref=ref, send_sem=far_send.at[dg], recv_sem=far_recv.at[dg],
+            device_id=(to_group, my_replica), device_id_type=MESH,
+        )
+
+    if extra:
+        pick = ones_at(iota((extra, rows), 0) + direct == spot, BF16)
+        got_rows[me, direct:slots] = jnp.dot(
+            pick, unit[...], preferred_element_type=F32
+        ).astype(BF16)
+    pack(order[0])
     pl.semaphore_wait(barrier, owners - 1)
+    if extra:
+        every(0, lambda dr: near_copy(peer(0, dr), me, dr).start())
+    every(order[0], lambda dr: start(row_bufs, order[0], dr))
+
+    high = jnp.floor(local * (1.0 / 32.0))
+    low = local - 32.0 * high
+    owned_d = jnp.where(rank < direct, owned_f, 0.0)
+    upper = lax.dot_general((owned_d * high).astype(BF16), place, NT, preferred_element_type=F32)
+    lower = lax.dot_general((owned_d * low).astype(BF16), place, NT, preferred_element_type=F32)
+    filled = lax.dot_general(owned_d.astype(BF16), place, NT, preferred_element_type=F32)
+    id_table = 32.0 * upper + lower + filled - 1.0
+    count = jnp.zeros((1, 1), F32)
+    if extra:
+        named = jnp.broadcast_to(late * (ids.astype(F32) + 1.0), (8, rows))
+        others = lax.dot_general(
+            named, place.astype(F32), NT, precision=EXACT, preferred_element_type=F32
+        )
+        id_table = id_table + others[0:1, :]
+        count = jnp.sum(late, axis=1, keepdims=True)
+    top = iota((8, LANES), 0) == 0
+    for o in range(owners):
+        send_ids[o] = jnp.where(top, id_table[o : o + 1, :], count)
+    got_ids[me] = send_ids[me]
+
     for dg in order:
         every(dg, lambda dr, dg=dg: start(id_bufs, dg, dr))
-    for dg in order:
-        tg = lax.rem(my_group + dg, groups)
-        pick = ones_at(iota((block, rows), 0) + tg * block == target, BF16)
-        packed = jnp.dot(pick, unit[...], preferred_element_type=F32).astype(BF16)
-        send_rows[pl.ds(tg * replicas, replicas)] = packed.reshape(replicas, slots, width)
+    for dg in order[1:]:
+        pack(dg)
         every(dg, lambda dr, dg=dg: start(row_bufs, dg, dr))
-    got_rows[me] = send_rows[me]
+    got_rows[me, 0:direct] = send_rows[me]
+    if extra:
+        def near_wait(dr):
+            pair = source(0, dr)
+            near_copy(pair, pair[0] * replicas + pair[1], dr).wait_recv()
+
+        every(0, near_wait)
+        for dg in order[:-1]:
+            far_copy(my_group, lax.rem(my_group + dg, groups), dg).start()
 
     for dg in order:
         every(dg, lambda dr, dg=dg: wait_recv(id_bufs, dg, dr))
+    worst = jnp.max(got_ids[:, 1, :], axis=0, keepdims=True)
+    over_ref[...] = jnp.where(worst > extra, 1, 0)
+    begin = jnp.sum(
+        jnp.where(iota((owners, 1), 0) == me, edges, 0), axis=0, keepdims=True
+    ).astype(F32)
+    ending = jnp.sum(
+        jnp.where(iota((owners, 1), 0) == me + 1, edges, 0), axis=0, keepdims=True
+    ).astype(F32) + jnp.where(me == owners - 1, float(CL_DEV * owners), 0.0)
 
     lane = iota((1, block), 1)
     quotient = jnp.zeros((1, block), jnp.int32)
@@ -159,6 +223,9 @@
     seen = jnp.zeros((limit, 1), F32)
     for sg in range(groups):
         table = got_ids[sg * replicas : (sg + 1) * replicas, 0, :]
+        if extra:
+            mine = jnp.where((table >= begin) & (table < ending), table - begin, -1.0)
+            table = jnp.where(iota((replicas, LANES), 1) < direct, table, mine)
         flat = jnp.sum(from_source * digits_dot(table, spread_b), axis=0, keepdims=True)
         mask = ones_at(cluster == flat.astype(jnp.int32), F32)
         mask_b = mask.astype(BF16)
@@ -173,6 +240,8 @@
     for dg in order:
         sg = lax.rem(my_group + groups - dg, groups)
         every(dg, lambda dr, dg=dg: wait_recv(row_bufs, dg, dr))
+        if extra and dg:
+            far_copy(sg, sg, dg).wait_recv()
         block_rows = got_rows[pl.ds(sg * replicas, replicas)].reshape(block, width)
         total[...] += jnp.dot(member[sg], block_rows, preferred_element_type=F32)
 
@@ -190,14 +259,13 @@
             from_source * (1.0 - near), spread_f, NT, precision=EXACT, preferred_element_type=F32
         )
         rank_mat = slot_mat[sg]
-        top = iota((8, LANES), 0) == 0
         for s in range(replicas):
             ret[tg * replicas + s] = jnp.where(top, dist_mat[s : s + 1, :], rank_mat[s : s + 1, :])
         back = (groups - dg) % groups
         every(back, lambda dr, back=back: start(ret_bufs, back, dr))
     got_ret[me] = ret[me]
 
-    place_f = ones_at(iota((LANES, rows), 0) == rank, F32)
+    place_f = ones_at(iota((LANES, rows), 0) == spot, F32)
     for dg in order:
         every(dg, lambda dr, dg=dg: wait_recv(ret_bufs, dg, dr))
     dist_all = jnp.dot(got_ret[:, 0, :], place_f, precision=EXACT, preferred_element_type=F32)
@@ -207,6 +275,10 @@
     for bufs in (id_bufs, row_bufs, ret_bufs):
         for dg in order:
             every(dg, lambda dr, dg=dg, bufs=bufs: wait_send(bufs, dg, dr))
+    if extra:
+        every(0, lambda dr: near_copy(peer(0, dr), me, dr).wait_send())
+        for dg in order[:-1]:
+            far_copy(my_group, lax.rem(my_group + dg, groups), dg).wait_send()
 
 
 def solution(mesh):
@@ -216,37 +288,54 @@
     def shards(embeddings, cluster_ids, owner_bounds):
         rows, width = embeddings.shape
         limit = CL_DEV + CL_DEV // 2
-        slots = -(-(3 * rows // owners) // 16) * 16
-        block = replicas * slots
+        most = -(-(3 * rows // owners) // 16) * 16
+        direct = -(-2 * most // 48) * 16
         vmem = pl.BlockSpec(memory_space=pltpu.VMEM)
         small = pltpu.VMEM((owners, 8, LANES), F32)
-        dma = pltpu.SemaphoreType.DMA((owners,))
-        centroids, distance, rank = pl.pallas_call(
-            functools.partial(kernel, groups, replicas, slots),
-            out_shape=(
-                jax.ShapeDtypeStruct((limit, width), BF16),
-                jax.ShapeDtypeStruct((1, rows), F32),
-                jax.ShapeDtypeStruct((1, rows), jnp.int32),
-            ),
-            in_specs=[vmem] * 3,
-            out_specs=(vmem,) * 3,
-            scratch_shapes=[
-                pltpu.VMEM((rows, width), BF16),
-                pltpu.VMEM((owners, slots, width), BF16),
-                pltpu.VMEM((owners, slots, width), BF16),
-                small,
-                small,
-                pltpu.VMEM((groups, limit, block), BF16),
-                pltpu.VMEM((limit, width), F32),
-                small,
-                small,
-                pltpu.VMEM((groups, replicas, LANES), F32),
-                dma, dma, dma, dma, dma, dma,
-            ],
-            compiler_params=pltpu.CompilerParams(
-                collective_id=0, has_side_effects=True, vmem_limit_bytes=56 * 1024 * 1024
-            ),
-        )(embeddings, cluster_ids.reshape(1, rows), owner_bounds.reshape(owners, 1))
+        each = pltpu.SemaphoreType.DMA((owners,))
+        near = pltpu.SemaphoreType.DMA((replicas,))
+        far = pltpu.SemaphoreType.DMA((groups,))
+        ids_row, edges = cluster_ids.reshape(1, rows), owner_bounds.reshape(owners, 1)
+
+        def run(direct, extra, number):
+            slots = direct + extra
+            return pl.pallas_call(
+                functools.partial(kernel, groups, replicas, direct, extra),
+                out_shape=(
+                    jax.ShapeDtypeStruct((limit, width), BF16),
+                    jax.ShapeDtypeStruct((1, rows), F32),
+                    jax.ShapeDtypeStruct((1, rows), jnp.int32),
+                    jax.ShapeDtypeStruct((1, LANES), jnp.int32),
+                ),
+                in_specs=[vmem] * 3,
+                out_specs=(vmem,) * 4,
+                scratch_shapes=[
+                    pltpu.VMEM((rows, width), BF16),
+                    pltpu.VMEM((owners, direct, width), BF16),
+                    pltpu.VMEM((owners, slots, width), BF16),
+                    small,
+                    small,
+                    pltpu.VMEM((groups, limit, replicas * slots), BF16),
+                    pltpu.VMEM((limit, width), F32),
+                    small,
+                    small,
+                    pltpu.VMEM((groups, replicas, LANES), F32),
+                    each, each, each, each, each, each, near, near, far, far,
+                ],
+                compiler_params=pltpu.CompilerParams(
+                    collective_id=number,
+                    has_side_effects=True,
+                    vmem_limit_bytes=48 * 1024 * 1024,
+                ),
+            )(embeddings, ids_row, edges)
+
+        if direct >= most:
+            centroids, distance, rank, _ = run(most, 0, 0)
+        else:
+            first = run(direct, most - direct, 0)
+            centroids, distance, rank = lax.cond(
+                first[3][0, 0] > 0, lambda: run(most, 0, 1)[:3], lambda: first[:3]
+            )
         return distance.reshape(rows), rank.reshape(rows), centroids[None]
 
     placed = (P(("grp", "rep"), None), P(("grp", "rep")), P())

time: 84 us -> 68.6 us (0.82)
  Pallas kernels: 77.7 us -> 64.1 us
  local copies, waits for them, and re-layouts: 5.36 us -> 3.55 us
    pallas_call x1, Pallas kernels: 77.7 us -> 64.1 us  [run(): pl.pallas_call(functools.partial(kernel, groups, replicas, direct, extra)...]
    unnamed x9, local copies, waits for them, and re-layouts: 4.67 us -> 2.74 us
where the time goes in v2:
time: 68.6 us; the launch traced here: 68.4 us
  Pallas kernels  64.1 us (93%)
  local copies, waits for them, and re-layouts  3.55 us (5%)
  between operations  0.71 us (1%)
    pallas_call x1, Pallas kernels, run(): pl.pallas_call(functools.partial(kernel, groups, replicas, direct, extra)...  64.1 us
    unnamed x9, local copies, waits for them, and re-layouts  2.74 us

profile of v2, /device:TPU:0, one launch (start us, length us, event | category | flops | bytes accessed | tf_op | source)
XLA Modules:
  0.0 68.4 jit_solution(12046658884333103642)
XLA Ops:
  0.6 0.0 copy-start
  0.6 0.8 %copy.6.bounds_ref = s32[32,1]{1,0:T(8,128)S(1)} copy(s32[32,1]{0,1:T(1,128)} %bitcast.15) | data formatting | bytes 256 | tf_op jit(solution)/shard_map/reshape | solution.py:298
  1.5 64.1 %shard_map.58 = (bf16[576,768]{1,0:T(8,128)(2,1)S(1)}, f32[1,512]{1,0:T(1,128)S(1)}, s32[1,512]{1,0:T(1,128)S(1)}, s32[1,128]{1,0:T(1,128)S(1)}) custom-call(bf16[512,768]{1,0:T(8,128)(2,1)} %emb_ref.1, s32[1,512]{1,0:T(1,128)} %bitcast.13, s32[32,1]{1,0:T(8,128)S(1)} %copy.6.bounds_ref), custom_call_target="tpu_custom_call" | custom-call | tf_op jit(solution)/shard_map/pallas_call | solution.py:302
  65.6 0.0 copy-start.1
  65.6 0.0 copy-start.2
  65.7 0.0 copy-done
  65.7 0.7 copy-done.1
  66.3 0.0 copy-done.2
  66.3 0.6 copy.20
  66.9 0.6 copy.21
  67.5 0.9 %copy.22 = bf16[1,576,768]{2,1,0:T(8,128)(2,1)} copy(bf16[1,576,768]{2,1,0:T(8,128)(2,1)S(1)} %get-tuple-element.76) | data formatting | bytes 1769472
  (1 shorter events, 0.0 us)
Async XLA Ops:
  0.6 65.0 %copy-start = (bf16[512,768]{1,0:T(8,128)(2,1)S(1)}, bf16[512,768]{1,0:T(8,128)(2,1)}, u32[]{:S(2)}) copy-start(bf16[512,768]{1,0:T(8,128)(2,1)} %emb_ref.1) | copy-start | bytes 2359300
  65.6 0.7 %copy-start.1 = (s32[512]{0:T(512)S(1)}, s32[512]{0:T(512)}, u32[]{:S(2)}) copy-start(s32[512]{0:T(512)} %param.6) | copy-start | bytes 6148
  65.6 0.7 copy-start.2
